TPU v7x, 256 devices: a whole 4x4x8 slice. The times are simulated.
256 devices in a mesh: dp: 16 (over z, y_lo), mp: 16 (over y_hi, x, core).
Axes of the slice: x: 4, y: 4 (y_hi: 2, y_lo: 2; y = y_hi * 2 + y_lo), z: 8, core: 2. Of those that a mesh axis runs over, the one named last changes fastest.
Arguments:
- gradient: bfloat16 [1, 4096, 4096], P(None, 'mp', 'dp'), may hold values from -6 to 6
- first_moment: float32 [1, 4096, 4096], P(None, 'mp', 'dp'), may hold values from -3 to 3
- second_moment: float32 [1, 4096, 4096], P(None, 'mp', 'dp'), may hold values from 0.0625 to 1
- left_factor: float32 [1, 4096, 4096], P(None, 'mp', 'dp'), may hold values from -18 to 18
- right_factor: float32 [1, 4096, 4096], P(None, 'mp', 'dp'), may hold values from -18 to 18
- left_basis: bfloat16 [1, 4096, 4096], P(None, 'dp', 'mp'), may hold values from -0.09375 to 0.09375
- right_basis: bfloat16 [1, 4096, 4096], P(None, 'mp', 'dp'), may hold values from -0.09375 to 0.09375
Outputs:
- new_first_moment: float32 [1, 4096, 4096], P(None, 'mp', 'dp')
- new_second_moment: float32 [1, 4096, 4096], P(None, 'mp', 'dp')
- new_left_factor: float32 [1, 4096, 4096], P(None, 'mp', 'dp')
- new_right_factor: float32 [1, 4096, 4096], P(None, 'mp', 'dp')
- update: bfloat16 [1, 4096, 4096], P(None, 'mp', 'dp')
All inputs are finite; a program needn't handle non-finite values.
Results may differ from a plain program's by a relative error of at most 0.014.
Values may be sent and summed in bfloat16 or wider, within the bound.
No kernel may reach another device: no remote copies, remote signals or barrier semaphores. Data moves between devices by JAX's collectives and lax.ppermute only.
A program may use at most 64 MiB of HBM per device.

v0:
```python
import jax
import jax.numpy as jnp
from jax import lax
from jax.sharding import PartitionSpec as P

decay_moment = 0.95
decay_factor = 0.95
epsilon = 1e-08


def in_one_piece(arrays, axis, dim, along):
    widths = [a.shape[along] for a in arrays]
    both = jnp.concatenate(arrays, axis=along)
    whole = lax.all_gather(both, axis, axis=dim, tiled=True)
    return tuple(jnp.split(whole, [sum(widths[:k]) for k in range(1, len(widths))], axis=along))


def turned_gather(arrays, axis, dims):
    turned = [jnp.moveaxis(a, dim, 0) for a, dim in zip(arrays, dims)]
    both = jnp.concatenate([t.reshape(len(t), -1) for t in turned], axis=1)
    whole, at, gathered = (lax.all_gather(both, axis, axis=0, tiled=True), 0, [])
    for t, dim in zip(turned, dims):
        section = whole[:, at : at + t[0].size].reshape(-1, *t.shape[1:])
        gathered.append(jnp.moveaxis(section, 0, dim))
        at += t[0].size
    return tuple(gathered)


def in_order(pieces, dim):
    lengths = list(pieces.shape[1:])
    lengths[dim] *= pieces.shape[0]
    return jnp.moveaxis(pieces, 0, dim).reshape(lengths)


def from_everyone(x, axis):
    length = lax.axis_size(axis)
    return lax.all_to_all(jnp.broadcast_to(x[None], (length, *x.shape)), axis, 0, 0, tiled=True)


def collect(x, axis, dim):
    return in_order(from_everyone(x, axis), dim)


def split_up(x, dim, length):
    lengths = x.shape
    pieces = x.reshape(*lengths[:dim], length, lengths[dim] // length, *lengths[dim + 1 :])
    return jnp.moveaxis(pieces, dim, 0)


def summed_on_arrival(x, axis, dim):
    pieces = split_up(x, dim, lax.axis_size(axis))
    arrived = lax.all_to_all(pieces, axis, split_axis=0, concat_axis=0, tiled=True)
    return arrived.astype(jnp.float32).sum(axis=0)


def per_device(
    gradient, first_moment, second_moment, left_factor, right_factor, left_basis, right_basis
):
    scale = 1.0 - decay_factor
    column_grad, column_right = in_one_piece((gradient, right_basis), "mp", 1, 0)
    row_grad, column_left = turned_gather((gradient, left_basis), "dp", (2, 1))
    row_block = lax.all_to_all(column_grad, "dp", split_axis=1, concat_axis=2, tiled=True)
    column_block = lax.all_to_all(row_grad, "mp", split_axis=2, concat_axis=1, tiled=True)
    left_sum = jnp.einsum("brc,bkc->brk", row_grad, row_block, preferred_element_type=jnp.float32)
    right_sum = jnp.einsum(
        "bkr,bkc->brc", column_block, column_grad, preferred_element_type=jnp.float32
    )
    rotated_left = jnp.einsum(
        "bkr,bkc->brc", column_left, column_grad, preferred_element_type=jnp.float32
    ).astype(jnp.bfloat16)
    rotated = jnp.einsum(
        "brn,bnc->brc",
        collect(rotated_left, "dp", 2),
        column_right,
        preferred_element_type=jnp.float32,
    )
    new_first = decay_moment * first_moment + (1.0 - decay_moment) * rotated
    new_second = decay_moment * second_moment + (1.0 - decay_moment) * rotated * rotated
    direction = (new_first / (jnp.sqrt(new_second) + epsilon)).astype(jnp.bfloat16)
    back_term = jnp.einsum(
        "bkr,brc->bkc", column_left, direction, preferred_element_type=jnp.float32
    )
    back_sum = summed_on_arrival(back_term.astype(jnp.bfloat16), "mp", 1)
    back_rows = back_sum.astype(jnp.bfloat16)
    update_term = jnp.einsum(
        "brc,bkc->brk", back_rows, column_right, preferred_element_type=jnp.float32
    )
    update_sum = summed_on_arrival(update_term.astype(jnp.bfloat16), "dp", 2)
    new_left = decay_factor * left_factor + scale * left_sum
    new_right = decay_factor * right_factor + scale * right_sum
    return (new_first, new_second, new_left, new_right, update_sum.astype(jnp.bfloat16))


def solution(mesh):
    in_specs = (
        P(None, "mp", "dp"),
        P(None, "mp", "dp"),
        P(None, "mp", "dp"),
        P(None, "mp", "dp"),
        P(None, "mp", "dp"),
        P(None, "dp", "mp"),
        P(None, "mp", "dp"),
    )
    out_specs = (
        P(None, "mp", "dp"),
        P(None, "mp", "dp"),
        P(None, "mp", "dp"),
        P(None, "mp", "dp"),
        P(None, "mp", "dp"),
    )
    return jax.shard_map(
        per_device, mesh=mesh, in_specs=in_specs, out_specs=out_specs, check_vma=False
    )
```

profile of v0, /device:TPU:16, one launch (start us, length us, event | category | flops | bytes accessed | tf_op | source)
XLA Modules:
  0.0 455.4 jit_solution(4310972106720529222)
XLA Ops:
  11.6 100.3 %all-gather.3.cloned.1.call-done = bf16[4096,512]{1,0:T(8,128)(2,1)} async-done(((bf16[256,512]{1,0:T(8,128)(2,1)}), bf16[4096,512]{1,0:T(8,128)(2,1)}) %all-gather.3.cloned.1.call-update) | async-done | bytes 4194320 | tf_op jit(solution)/shard_map/all_gather | solution.py:21
  112.0 62.4 %all-gather.5.cloned.1.call-done = bf16[2,4096,256]{2,1,0:T(8,128)(2,1)} async-done(((bf16[2,256,256]{2,1,0:T(8,128)(2,1)}), bf16[2,4096,256]{2,1,0:T(8,128)(2,1)}) %all-gather.5.cloned.1.call-update) | async-done | bytes 4194320 | tf_op jit(solution)/shard_map/all_gather | solution.py:14
  174.4 3.0 fusion.28
  179.0 8.7 %all-to-all-start = ((bf16[16,1,256,256]{2,3,1,0:T(8,128)(2,1)}), bf16[16,1,256,256]{2,3,1,0:T(8,128)(2,1)}, u32[]{:S(2)}, u32[]{:S(2)}) async-start(bf16[16,1,256,256]{2,3,1,0:T(8,128)(2,1)} %broadcast_in_dim.2), calls=%async_computation | async-start | bytes 4194304 | tf_op jit(solution)/shard_map/all_to_all | solution.py:37
  189.4 25.0 %copy.45 = bf16[1,256,4096]{1,0,2:T(2,128)(2,1)} copy(bf16[1,256,4096]{1,2,0:T(8,128)(2,1)S(1)} %slice_bitcast_fusion.3) | data formatting | bytes 4194304 | tf_op jit(solution)/shard_map/transpose | solution.py:24
  215.0 21.6 %reduce.5 = bf16[4096,256]{1,0:T(8,128)(2,1)S(1)} reduce(bf16[4096,1,256]{2,1,0:T(2,128)(2,1)} %bitcast.92, bf16[]{:T(256)} %broadcast.21), dimensions={1}, to_apply=%bitcast.90.reduce_sub_computation | reduce | bytes 4194306
  238.7 6.8 %all-to-all-start.2 = ((bf16[16,2,32768]{2,1,0:T(2,128)(2,1)}), bf16[16,2,32768]{2,1,0:T(2,128)(2,1)S(1)}, u32[]{:S(2)}, u32[]{:S(2)}) async-start(bf16[16,2,32768]{2,1,0:T(2,128)(2,1)} %reshape.85), calls=%async_computation.2 | async-start | bytes 4194304 | tf_op jit(solution)/shard_map/all_to_all | solution.py:63
  245.5 3.1 fusion.35
  251.0 21.6 %all-to-all-done.2 = bf16[16,2,32768]{2,1,0:T(2,128)(2,1)S(1)} async-done(((bf16[16,2,32768]{2,1,0:T(2,128)(2,1)}), bf16[16,2,32768]{2,1,0:T(2,128)(2,1)S(1)}, u32[]{:S(2)}, u32[]{:S(2)}) %all-to-all-start.2) | async-done | bytes 2097184 | tf_op jit(solution)/shard_map/all_to_all | solution.py:63
  272.6 6.6 %all-to-all-start.3 = ((bf16[16,1,256,256]{3,2,1,0:T(8,128)(2,1)}), bf16[16,1,256,256]{3,2,1,0:T(8,128)(2,1)}, u32[]{:S(2)}, u32[]{:S(2)}) async-start(bf16[16,1,256,256]{3,2,1,0:T(8,128)(2,1)} %bitcast.101), calls=%async_computation.3 | async-start | bytes 4194304 | tf_op jit(solution)/shard_map/all_to_all | solution.py:52
  280.8 25.0 %copy.46 = bf16[1,4096,256]{2,0,1:T(2,128)(2,1)} copy(bf16[1,4096,256]{2,1,0:T(8,128)(2,1)S(1)} %slice-done) | data formatting | bytes 4194304 | tf_op jit(solution)/shard_map/split | solution.py:15
  305.8 22.9 %reduce.4 = bf16[4096,256]{1,0:T(8,128)(2,1)} reduce(bf16[4096,1,256]{2,1,0:T(2,128)(2,1)} %bitcast.93, bf16[]{:T(256)} %broadcast.21), dimensions={1}, to_apply=%bitcast.91.reduce_sub_computation | reduce | bytes 4194306
  328.8 4.0 reshape.83
  332.7 8.1 %all-to-all-start.1 = ((bf16[16,2,32768]{2,1,0:T(2,128)(2,1)}), bf16[16,2,32768]{2,1,0:T(2,128)(2,1)}, u32[]{:S(2)}, u32[]{:S(2)}) async-start(bf16[16,2,32768]{2,1,0:T(2,128)(2,1)} %reshape.83), calls=%async_computation.1 | async-start | bytes 4194304 | tf_op jit(solution)/shard_map/all_to_all | solution.py:62
  347.8 43.6 %all-to-all-done.1 = bf16[16,2,32768]{2,1,0:T(2,128)(2,1)} async-done(((bf16[16,2,32768]{2,1,0:T(2,128)(2,1)}), bf16[16,2,32768]{2,1,0:T(2,128)(2,1)}, u32[]{:S(2)}, u32[]{:S(2)}) %all-to-all-start.1) | async-done | bytes 2097184 | tf_op jit(solution)/shard_map/all_to_all | solution.py:62
  391.4 4.7 %all-to-all-start.4 = ((bf16[16,1,256,256]{3,2,1,0:T(8,128)(2,1)}), bf16[16,1,256,256]{3,2,1,0:T(8,128)(2,1)}, u32[]{:S(2)}, u32[]{:S(2)}) async-start(bf16[16,1,256,256]{3,2,1,0:T(8,128)(2,1)} %bitcast.98), calls=%async_computation.4 | async-start | bytes 4194304 | tf_op jit(solution)/shard_map/all_to_all | solution.py:52
  396.1 6.8 %reshape.86 = bf16[4096,1,256]{2,1,0:T(2,128)(2,1)} reshape(bf16[16,2,32768]{2,1,0:T(2,128)(2,1)S(1)} %all-to-all-done.2) | data formatting | bytes 4194304
  402.9 2.5 copy.39
  408.0 3.7 fusion.25
  411.6 10.5 %reshape.84 = bf16[4096,1,256]{2,1,0:T(2,128)(2,1)} reshape(bf16[16,2,32768]{2,1,0:T(2,128)(2,1)} %all-to-all-done.1) | data formatting | bytes 4194304
  422.1 2.5 copy.38
  427.1 3.7 fusion.22
  430.8 15.2 %all-to-all-done.4 = bf16[16,1,256,256]{3,2,1,0:T(8,128)(2,1)} async-done(((bf16[16,1,256,256]{3,2,1,0:T(8,128)(2,1)}), bf16[16,1,256,256]{3,2,1,0:T(8,128)(2,1)}, u32[]{:S(2)}, u32[]{:S(2)}) %all-to-all-start.4) | async-done | bytes 2097184 | tf_op jit(solution)/shard_map/all_to_all | solution.py:52
  445.9 2.6 reduce_sum.27
  (37 shorter events, 26.2 us)
Async XLA Ops:
  7.2 104.8 %all-gather.3.cloned.1.call-start = ((), (), s32[]{:S(2)}) async-start(), calls=%async_computation.5 | async-start | bytes 4456448 | tf_op jit(solution)/shard_map/all_gather | solution.py:21
  9.9 164.5 %all-gather.5.cloned.1.call-start = ((), (), s32[]{:S(2)}) async-start(), calls=%async_computation.6 | async-start | bytes 4456448 | tf_op jit(solution)/shard_map/all_gather | solution.py:14
  179.0 59.7 %all-to-all-start = ((bf16[16,1,256,256]{2,3,1,0:T(8,128)(2,1)}), bf16[16,1,256,256]{2,3,1,0:T(8,128)(2,1)}, u32[]{:S(2)}, u32[]{:S(2)}) async-start(bf16[16,1,256,256]{2,3,1,0:T(8,128)(2,1)} %broadcast_in_dim.2), calls=%async_computation | async-start | bytes 4194304 | tf_op jit(solution)/shard_map/all_to_all | solution.py:37
  238.7 6.8 %copy-start.1 = (f32[1,256,256]{2,1,0:T(8,128)S(1)}, f32[1,256,256]{2,1,0:T(8,128)}, u32[]{:S(2)}) copy-start(f32[1,256,256]{2,1,0:T(8,128)} %param.9) | copy-start | bytes 786436
  238.7 6.8 %copy-start.2 = (f32[1,256,256]{2,1,0:T(8,128)S(1)}, f32[1,256,256]{2,1,0:T(8,128)}, u32[]{:S(2)}) copy-start(f32[1,256,256]{2,1,0:T(8,128)} %param.8) | copy-start | bytes 786436
  238.7 33.9 %all-to-all-start.2 = ((bf16[16,2,32768]{2,1,0:T(2,128)(2,1)}), bf16[16,2,32768]{2,1,0:T(2,128)(2,1)S(1)}, u32[]{:S(2)}, u32[]{:S(2)}) async-start(bf16[16,2,32768]{2,1,0:T(2,128)(2,1)} %reshape.85), calls=%async_computation.2 | async-start | bytes 4194304 | tf_op jit(solution)/shard_map/all_to_all | solution.py:63
  245.5 3.5 copy-start
  248.6 2.4 copy-start.5
  248.6 2.4 copy-start.6
  272.6 60.1 %all-to-all-start.3 = ((bf16[16,1,256,256]{3,2,1,0:T(8,128)(2,1)}), bf16[16,1,256,256]{3,2,1,0:T(8,128)(2,1)}, u32[]{:S(2)}, u32[]{:S(2)}) async-start(bf16[16,1,256,256]{3,2,1,0:T(8,128)(2,1)} %bitcast.101), calls=%async_computation.3 | async-start | bytes 4194304 | tf_op jit(solution)/shard_map/all_to_all | solution.py:52
  279.2 1.6 slice-start
  332.7 58.7 %all-to-all-start.1 = ((bf16[16,2,32768]{2,1,0:T(2,128)(2,1)}), bf16[16,2,32768]{2,1,0:T(2,128)(2,1)}, u32[]{:S(2)}, u32[]{:S(2)}) async-start(bf16[16,2,32768]{2,1,0:T(2,128)(2,1)} %reshape.83), calls=%async_computation.1 | async-start | bytes 4194304 | tf_op jit(solution)/shard_map/all_to_all | solution.py:62
  391.4 54.5 %all-to-all-start.4 = ((bf16[16,1,256,256]{3,2,1,0:T(8,128)(2,1)}), bf16[16,1,256,256]{3,2,1,0:T(8,128)(2,1)}, u32[]{:S(2)}, u32[]{:S(2)}) async-start(bf16[16,1,256,256]{3,2,1,0:T(8,128)(2,1)} %bitcast.98), calls=%async_computation.4 | async-start | bytes 4194304 | tf_op jit(solution)/shard_map/all_to_all | solution.py:52
  405.5 2.5 copy-start.3
  424.7 2.4 copy-start.4
Sparse Core Ops, SparseCore 0:
  10.3 101.6 all-gather.2
  115.3 59.0 all-gather.4
where the time goes:
time: 456 us; the launch traced here: 455 us
  waiting for transfers between devices  243 us (53%)
  local copies, waits for them, and re-layouts  92.9 us (20%)
  other arithmetic  52.3 us (11%)
  starting transfers between devices  35 us (8%)
  matrix products  17.8 us (4%)
  between operations  14.2 us (3%)
    all_gather x1, waiting for transfers between devices, turned_gather(): lax.all_gather(both, axis, axis=0, tiled=True)  100 us
    all_gather x1, waiting for transfers between devices, in_one_piece(): whole = lax.all_gather(both, axis, axis=dim, tiled=True)  62.4 us
    unnamed x2, other arithmetic  44.5 us
    all_to_all x1, waiting for transfers between devices, per_device(): lax.all_to_all(column_grad, 'dp', split_axis=1, concat_axis=2, tiled=True)  43.6 us
    unnamed x23, local copies, waits for them, and re-layouts  31 us
    transpose x2, local copies, waits for them, and re-layouts, turned_gather(): gathered.append(jnp.moveaxis(section, 0, dim))  26.8 us
    split x3, local copies, waits for them, and re-layouts, in_one_piece(): jnp.split(whole, [sum(widths[:k]) for k in range(1, len(widths))], axis=a...  26.6 us
    all_to_all x1, waiting for transfers between devices, per_device(): lax.all_to_all(row_grad, 'mp', split_axis=2, concat_axis=1, tiled=True)  21.6 us
  transfers between devices with their start and end apart: 7, of which 5 were waited for; matrix products, arithmetic and copies ran while one was open for 33% of the time, Pallas kernels for 0%

commit v1 on v0

--- a/solution.py
+++ b/solution.py
@@ -6,6 +6,11 @@
 decay_moment = 0.95
 decay_factor = 0.95
 epsilon = 1e-08
+
+
+def exchange_gather(array, name, dim):
+    outgoing = jnp.stack([array] * lax.axis_size(name))
+    return jnp.concatenate(lax.all_to_all(outgoing, name, 0, 0), axis=dim)
 
 
 def in_one_piece(arrays, axis, dim, along):
@@ -18,7 +23,7 @@
 def turned_gather(arrays, axis, dims):
     turned = [jnp.moveaxis(a, dim, 0) for a, dim in zip(arrays, dims)]
     both = jnp.concatenate([t.reshape(len(t), -1) for t in turned], axis=1)
-    whole, at, gathered = (lax.all_gather(both, axis, axis=0, tiled=True), 0, [])
+    whole, at, gathered = (exchange_gather(both, axis, 0), 0, [])
     for t, dim in zip(turned, dims):
         section = whole[:, at : at + t[0].size].reshape(-1, *t.shape[1:])
         gathered.append(jnp.moveaxis(section, 0, dim))

time: 456 us -> 399 us (0.88)
  waiting for transfers between devices: 243 us -> 177 us
  starting transfers between devices: 35 us -> 41.2 us
    all_gather x1 -> x0, waiting for transfers between devices: 100 us -> none  [turned_gather(): lax.all_gather(both, axis, axis=0, tiled=True)]
    all_to_all x0 -> x1, waiting for transfers between devices: none -> 46.1 us  [exchange_gather(): return jnp.concatenate(lax.all_to_all(outgoing, name, 0, 0), axis=dim)]
    all_gather x1, waiting for transfers between devices: 62.4 us -> 51.3 us  [in_one_piece(): whole = lax.all_gather(both, axis, axis=dim, tiled=True)]
    all_to_all x0 -> x1, starting transfers between devices: none -> 9.34 us  [exchange_gather(): return jnp.concatenate(lax.all_to_all(outgoing, name, 0, 0), axis=dim)]
    unnamed x23 -> x21, local copies, waits for them, and re-layouts: 31 us -> 30.7 us
  transfers between devices with their start and end apart: 7 -> 7, of which waited for: 5 -> 5; matrix products, arithmetic and copies ran while one was open for 33% -> 39% of each run, Pallas kernels for 0% -> 0%
where the time goes in v1:
time: 399 us; the launch traced here: 398 us
  waiting for transfers between devices  177 us (44%)
  local copies, waits for them, and re-layouts  94.9 us (24%)
  other arithmetic  51.6 us (13%)
  starting transfers between devices  41.2 us (10%)
  matrix products  19.4 us (5%)
  between operations  14.2 us (4%)
    all_gather x1, waiting for transfers between devices, in_one_piece(): whole = lax.all_gather(both, axis, axis=dim, tiled=True)  51.3 us
    all_to_all x1, waiting for transfers between devices, exchange_gather(): return jnp.concatenate(lax.all_to_all(outgoing, name, 0, 0), axis=dim)  46.1 us
    unnamed x2, other arithmetic  44.5 us
    all_to_all x1, waiting for transfers between devices, per_device(): lax.all_to_all(column_grad, 'dp', split_axis=1, concat_axis=2, tiled=True)  43.6 us
    unnamed x21, local copies, waits for them, and re-layouts  30.7 us
    transpose x2, local copies, waits for them, and re-layouts, turned_gather(): gathered.append(jnp.moveaxis(section, 0, dim))  26.8 us
    split x3, local copies, waits for them, and re-layouts, in_one_piece(): jnp.split(whole, [sum(widths[:k]) for k in range(1, len(widths))], axis=a...  26.6 us
    all_to_all x1, waiting for transfers between devices, per_device(): lax.all_to_all(row_grad, 'mp', split_axis=2, concat_axis=1, tiled=True)  20.3 us
  transfers between devices with their start and end apart: 7, of which 5 were waited for; matrix products, arithmetic and copies ran while one was open for 39% of the time, Pallas kernels for 0%

profile of v1, /device:TPU:16, one launch (start us, length us, event | category | flops | bytes accessed | tf_op | source)
XLA Modules:
  0.0 397.9 jit_solution(11445842321485780609)
XLA Ops:
  13.2 9.3 %all-to-all-start = ((bf16[16,256,512]{2,1,0:T(8,128)(2,1)}), bf16[16,256,512]{2,1,0:T(8,128)(2,1)}, u32[]{:S(2)}, u32[]{:S(2)}) async-start(bf16[16,256,512]{2,1,0:T(8,128)(2,1)} %stack.2), calls=%async_computation | async-start | bytes 8388608 | tf_op jit(solution)/shard_map/all_to_all | solution.py:13
  22.6 51.3 %all-gather.2.cloned.1.call-done = bf16[2,4096,256]{2,1,0:T(8,128)(2,1)} async-done(((bf16[2,256,256]{2,1,0:T(8,128)(2,1)}), bf16[2,4096,256]{2,1,0:T(8,128)(2,1)}) %all-gather.2.cloned.1.call-update) | async-done | bytes 4194320 | tf_op jit(solution)/shard_map/all_gather | solution.py:19
  73.9 46.1 %all-to-all-done = bf16[16,256,512]{2,1,0:T(8,128)(2,1)} async-done(((bf16[16,256,512]{2,1,0:T(8,128)(2,1)}), bf16[16,256,512]{2,1,0:T(8,128)(2,1)}, u32[]{:S(2)}, u32[]{:S(2)}) %all-to-all-start) | async-done | bytes 4194336 | tf_op jit(solution)/shard_map/all_to_all | solution.py:13
  120.0 3.0 fusion.28
  124.6 5.0 %all-to-all-start.1 = ((bf16[16,1,256,256]{2,3,1,0:T(8,128)(2,1)}), bf16[16,1,256,256]{2,3,1,0:T(8,128)(2,1)}, u32[]{:S(2)}, u32[]{:S(2)}) async-start(bf16[16,1,256,256]{2,3,1,0:T(8,128)(2,1)} %broadcast_in_dim.2), calls=%async_computation.1 | async-start | bytes 4194304 | tf_op jit(solution)/shard_map/all_to_all | solution.py:42
  131.4 25.0 %copy.45 = bf16[1,256,4096]{1,0,2:T(2,128)(2,1)} copy(bf16[1,256,4096]{1,2,0:T(8,128)(2,1)S(1)} %slice_bitcast_fusion.3) | data formatting | bytes 4194304 | tf_op jit(solution)/shard_map/transpose | solution.py:29
  156.9 21.6 %reduce.5 = bf16[4096,256]{1,0:T(8,128)(2,1)S(1)} reduce(bf16[4096,1,256]{2,1,0:T(2,128)(2,1)} %bitcast.93, bf16[]{:T(256)} %broadcast.23), dimensions={1}, to_apply=%bitcast.91.reduce_sub_computation | reduce | bytes 4194306
  180.6 7.4 %all-to-all-start.3 = ((bf16[16,2,32768]{2,1,0:T(2,128)(2,1)}), bf16[16,2,32768]{2,1,0:T(2,128)(2,1)S(1)}, u32[]{:S(2)}, u32[]{:S(2)}) async-start(bf16[16,2,32768]{2,1,0:T(2,128)(2,1)} %reshape.91), calls=%async_computation.3 | async-start | bytes 4194304 | tf_op jit(solution)/shard_map/all_to_all | solution.py:68
  188.1 3.0 fusion.35
  191.1 3.8 convolution_convert_fusion.1
  194.9 20.3 %all-to-all-done.3 = bf16[16,2,32768]{2,1,0:T(2,128)(2,1)S(1)} async-done(((bf16[16,2,32768]{2,1,0:T(2,128)(2,1)}), bf16[16,2,32768]{2,1,0:T(2,128)(2,1)S(1)}, u32[]{:S(2)}, u32[]{:S(2)}) %all-to-all-start.3) | async-done | bytes 2097184 | tf_op jit(solution)/shard_map/all_to_all | solution.py:68
  215.2 6.6 %all-to-all-start.4 = ((bf16[16,1,256,256]{3,2,1,0:T(8,128)(2,1)}), bf16[16,1,256,256]{3,2,1,0:T(8,128)(2,1)}, u32[]{:S(2)}, u32[]{:S(2)}) async-start(bf16[16,1,256,256]{3,2,1,0:T(8,128)(2,1)} %bitcast.102), calls=%async_computation.4 | async-start | bytes 4194304 | tf_op jit(solution)/shard_map/all_to_all | solution.py:57
  223.4 25.0 %copy.46 = bf16[1,4096,256]{2,0,1:T(2,128)(2,1)} copy(bf16[1,4096,256]{2,1,0:T(8,128)(2,1)S(1)} %slice-done) | data formatting | bytes 4194304 | tf_op jit(solution)/shard_map/split | solution.py:20
  248.4 22.9 %reduce.4 = bf16[4096,256]{1,0:T(8,128)(2,1)} reduce(bf16[4096,1,256]{2,1,0:T(2,128)(2,1)} %bitcast.94, bf16[]{:T(256)} %broadcast.23), dimensions={1}, to_apply=%bitcast.92.reduce_sub_computation | reduce | bytes 4194306
  271.3 4.0 %reshape.89 = bf16[16,2,32768]{2,1,0:T(2,128)(2,1)} reshape(bf16[4096,256]{1,0:T(8,128)(2,1)} %reduce.4) | data formatting | bytes 4194304
  275.3 8.1 %all-to-all-start.2 = ((bf16[16,2,32768]{2,1,0:T(2,128)(2,1)}), bf16[16,2,32768]{2,1,0:T(2,128)(2,1)}, u32[]{:S(2)}, u32[]{:S(2)}) async-start(bf16[16,2,32768]{2,1,0:T(2,128)(2,1)} %reshape.89), calls=%async_computation.2 | async-start | bytes 4194304 | tf_op jit(solution)/shard_map/all_to_all | solution.py:67
  290.4 43.6 %all-to-all-done.2 = bf16[16,2,32768]{2,1,0:T(2,128)(2,1)} async-done(((bf16[16,2,32768]{2,1,0:T(2,128)(2,1)}), bf16[16,2,32768]{2,1,0:T(2,128)(2,1)}, u32[]{:S(2)}, u32[]{:S(2)}) %all-to-all-start.2) | async-done | bytes 2097184 | tf_op jit(solution)/shard_map/all_to_all | solution.py:67
  334.0 4.7 %all-to-all-start.5 = ((bf16[16,1,256,256]{3,2,1,0:T(8,128)(2,1)}), bf16[16,1,256,256]{3,2,1,0:T(8,128)(2,1)}, u32[]{:S(2)}, u32[]{:S(2)}) async-start(bf16[16,1,256,256]{3,2,1,0:T(8,128)(2,1)} %bitcast.99), calls=%async_computation.5 | async-start | bytes 4194304 | tf_op jit(solution)/shard_map/all_to_all | solution.py:57
  338.7 6.8 %reshape.92 = bf16[4096,1,256]{2,1,0:T(2,128)(2,1)} reshape(bf16[16,2,32768]{2,1,0:T(2,128)(2,1)S(1)} %all-to-all-done.3) | data formatting | bytes 4194304
  350.5 3.7 fusion.25
  354.2 10.5 %reshape.90 = bf16[4096,1,256]{2,1,0:T(2,128)(2,1)} reshape(bf16[16,2,32768]{2,1,0:T(2,128)(2,1)} %all-to-all-done.2) | data formatting | bytes 4194304
  369.6 3.7 fusion.22
  373.3 15.2 %all-to-all-done.5 = bf16[16,1,256,256]{3,2,1,0:T(8,128)(2,1)} async-done(((bf16[16,1,256,256]{3,2,1,0:T(8,128)(2,1)}), bf16[16,1,256,256]{3,2,1,0:T(8,128)(2,1)}, u32[]{:S(2)}, u32[]{:S(2)}) %all-to-all-start.5) | async-done | bytes 2097184 | tf_op jit(solution)/shard_map/all_to_all | solution.py:57
  388.5 2.6 reduce_sum.27
  (35 shorter events, 30.5 us)
Async XLA Ops:
  7.2 66.8 %all-gather.2.cloned.1.call-start = ((), (), s32[]{:S(2)}) async-start(), calls=%async_computation.6 | async-start | bytes 4456448 | tf_op jit(solution)/shard_map/all_gather | solution.py:19
  13.2 106.8 %all-to-all-start = ((bf16[16,256,512]{2,1,0:T(8,128)(2,1)}), bf16[16,256,512]{2,1,0:T(8,128)(2,1)}, u32[]{:S(2)}, u32[]{:S(2)}) async-start(bf16[16,256,512]{2,1,0:T(8,128)(2,1)} %stack.2), calls=%async_computation | async-start | bytes 8388608 | tf_op jit(solution)/shard_map/all_to_all | solution.py:13
  124.6 56.0 %all-to-all-start.1 = ((bf16[16,1,256,256]{2,3,1,0:T(8,128)(2,1)}), bf16[16,1,256,256]{2,3,1,0:T(8,128)(2,1)}, u32[]{:S(2)}, u32[]{:S(2)}) async-start(bf16[16,1,256,256]{2,3,1,0:T(8,128)(2,1)} %broadcast_in_dim.2), calls=%async_computation.1 | async-start | bytes 4194304 | tf_op jit(solution)/shard_map/all_to_all | solution.py:42
  180.6 7.4 %copy-start = (f32[1,256,256]{2,1,0:T(8,128)S(1)}, f32[1,256,256]{2,1,0:T(8,128)}, u32[]{:S(2)}) copy-start(f32[1,256,256]{2,1,0:T(8,128)} %param.9) | copy-start | bytes 786436
  180.6 7.4 %copy-start.1 = (f32[1,256,256]{2,1,0:T(8,128)S(1)}, f32[1,256,256]{2,1,0:T(8,128)}, u32[]{:S(2)}) copy-start(f32[1,256,256]{2,1,0:T(8,128)} %param.8) | copy-start | bytes 786436
  180.6 34.5 %all-to-all-start.3 = ((bf16[16,2,32768]{2,1,0:T(2,128)(2,1)}), bf16[16,2,32768]{2,1,0:T(2,128)(2,1)S(1)}, u32[]{:S(2)}, u32[]{:S(2)}) async-start(bf16[16,2,32768]{2,1,0:T(2,128)(2,1)} %reshape.91), calls=%async_computation.3 | async-start | bytes 4194304 | tf_op jit(solution)/shard_map/all_to_all | solution.py:68
  191.0 3.9 copy-start.4
  191.0 3.9 copy-start.5
  215.2 60.1 %all-to-all-start.4 = ((bf16[16,1,256,256]{3,2,1,0:T(8,128)(2,1)}), bf16[16,1,256,256]{3,2,1,0:T(8,128)(2,1)}, u32[]{:S(2)}, u32[]{:S(2)}) async-start(bf16[16,1,256,256]{3,2,1,0:T(8,128)(2,1)} %bitcast.102), calls=%async_computation.4 | async-start | bytes 4194304 | tf_op jit(solution)/shard_map/all_to_all | solution.py:57
  221.8 1.6 slice-start
  275.3 58.7 %all-to-all-start.2 = ((bf16[16,2,32768]{2,1,0:T(2,128)(2,1)}), bf16[16,2,32768]{2,1,0:T(2,128)(2,1)}, u32[]{:S(2)}, u32[]{:S(2)}) async-start(bf16[16,2,32768]{2,1,0:T(2,128)(2,1)} %reshape.89), calls=%async_computation.2 | async-start | bytes 4194304 | tf_op jit(solution)/shard_map/all_to_all | solution.py:67
  334.0 54.5 %all-to-all-start.5 = ((bf16[16,1,256,256]{3,2,1,0:T(8,128)(2,1)}), bf16[16,1,256,256]{3,2,1,0:T(8,128)(2,1)}, u32[]{:S(2)}, u32[]{:S(2)}) async-start(bf16[16,1,256,256]{3,2,1,0:T(8,128)(2,1)} %bitcast.99), calls=%async_computation.5 | async-start | bytes 4194304 | tf_op jit(solution)/shard_map/all_to_all | solution.py:57
  348.0 2.5 copy-start.2
  367.2 2.4 copy-start.3
Sparse Core Ops, SparseCore 0:
  11.3 62.5 all-gather.1
